TPU v7x, 128 devices: a whole 4x4x4 slice. The times are simulated.
128 devices in a mesh: band: 32 (over z, y_hi, x), gvec: 4 (over y_lo, core).
Axes of the slice: x: 4, y: 4 (y_hi: 2, y_lo: 2; y = y_hi * 2 + y_lo), z: 4, core: 2. Of those that a mesh axis runs over, the one named last changes fastest.
Arguments:
- wave_coeffs: bfloat16 [2, 1024, 75264], P(None, 'band', 'gvec'), may hold values from -6 to 6
- projectors: bfloat16 [2, 256, 75264], P(None, 'band', 'gvec'), may hold values from -0.0234375 to 0.0234375
- miller_index: int32 [3, 75264], P(None, 'gvec'), may hold values from -24 to 24
- lattice: float32 [3, 3], replicated, may hold values from -0.25 to 1.25
- occupation: float32 [1024], P('band'), may hold values from 0 to 2
- species: int32 [32], replicated, may hold values from 0 to 3
- proj_count: int32 [32], replicated, may hold values from 4 to 8
- coupling: float32 [4, 8, 8], replicated, may hold values from -0.4 to 2, as said below
Outputs:
- forces: float32 [3, 32], P(None, 'band')
- stress: float32 [3, 3], replicated
Inputs may be any that keep to these rules, and one draw needn't show every extreme that they name: `coupling`: symmetric in its last two dimensions.
All inputs are finite; a program needn't handle non-finite values.
Results may differ from a plain program's by a relative error of at most 0.006.
Values may be sent and summed in bfloat16 or wider, within the bound.
A program may use at most 64 MiB of HBM per device.

v0:
```python
import math

import jax
import jax.numpy as jnp
from jax import lax
from jax.sharding import Mesh
from jax.sharding import PartitionSpec as P

PROJ = 8
MILLER = 24
GVEC = ("gvec_0", "gvec_1")
BAND = ("band_0", "band_1", "band_2")
BAND_GVEC = ("band_0", "band_1", "band_2", "gvec_0", "gvec_1")


stress_pairs = ((0, 0), (1, 1), (2, 2), (0, 1), (0, 2), (1, 2))


def split_up(array, dim, count):
    before, after = (array.shape[:dim], array.shape[dim + 1 :])
    return jnp.moveaxis(array.reshape(*before, count, -1, *after), dim, 0)


def sent_and_summed(array, axis, dim):
    count = lax.axis_size(axis)
    parts = lax.all_to_all(split_up(array, dim, count), axis, 0, 0, tiled=True)
    return jnp.sum(parts.astype(jnp.float32), axis=0)


def from_everyone(array, axis):
    count = lax.axis_size(axis)
    return lax.all_to_all(
        jnp.broadcast_to(array[None], (count, *array.shape)), axis, 0, 0, tiled=True
    )


def taken_together(array, axis):
    everything = from_everyone(array, axis)
    return jnp.sum(everything, axis=0)


def sum_at_owner(array, axis, dim):
    count = lax.axis_size(axis)
    parts = lax.all_to_all(split_up(array, dim, count), axis, 0, 0, tiled=True)
    return jnp.sum(parts, axis=0)


def one_axis_at_a_time(array, axes):
    for axis in axes:
        array = lax.psum(array, axis)
    return array


def cart_weights(miller_index, lattice):
    indices = miller_index.astype(jnp.float32)
    coords = []
    for column in range(3):
        coords.append(
            (
                indices[0] * lattice[0, column]
                + indices[1] * lattice[1, column]
                + indices[2] * lattice[2, column]
            )
            / MILLER
        )
    isotropic = (coords[0] * coords[0] + coords[1] * coords[1] + coords[2] * coords[2]) / 3.0
    weight_rows = [jnp.ones_like(coords[0])] + coords
    for first_axis, second_axis in stress_pairs:
        product = coords[first_axis] * coords[second_axis]
        if first_axis == second_axis:
            product = product - isotropic
        weight_rows.append(product)
    return jnp.stack(weight_rows)


def scale_block(weights, atom_block):
    proj_rows = atom_block.shape[1]
    scaled = (weights[:, None, None, :] * atom_block[None].astype(jnp.float32)).astype(jnp.bfloat16)
    return scaled.reshape(20 * proj_rows, atom_block.shape[2])


def intersection(scaled, flat_waves):
    product = lax.dot_general(
        scaled, flat_waves, (((1,), (1,)), ((), ())), preferred_element_type=jnp.float32
    )
    product = product.reshape(10, 2, scaled.shape[0] // 20, 2, flat_waves.shape[0] // 2)
    real_part = product[:, 0, :, 0] + product[:, 1, :, 1]
    imag_part = product[:, 0, :, 1] - product[:, 1, :, 0]
    return jnp.stack([real_part, imag_part], axis=1)


def atom_couplings(species, proj_count, coupling):
    kind_count = coupling.shape[0]
    proj_width = coupling.shape[1]
    onehot = (species[:, None] == jnp.arange(kind_count, dtype=jnp.int32)[None, :]).astype(
        jnp.float32
    )
    chosen = jnp.einsum("as,sij->aij", onehot, coupling, precision=lax.Precision.HIGHEST)
    active = (jnp.arange(proj_width, dtype=jnp.int32)[None, :] < proj_count[:, None]).astype(
        jnp.float32
    )
    return chosen * active[:, :, None] * active[:, None, :]


def contract(per_atom, couplings, occupied):
    mixed = jnp.einsum("aij,kcajn->kcain", couplings, per_atom, precision=lax.Precision.HIGHEST)
    becp_real = per_atom[0, 0]
    becp_imag = per_atom[0, 1]
    imag_sum = jnp.sum(becp_real[None] * mixed[1:4, 1] - becp_imag[None] * mixed[1:4, 0], axis=2)
    real_sum = jnp.sum(becp_real[None] * mixed[4:, 0] + becp_imag[None] * mixed[4:, 1], axis=2)
    force_part = jnp.sum(imag_sum * occupied, axis=2)
    stress_part = jnp.sum(real_sum * occupied, axis=(1, 2))
    return (force_part, stress_part)


def stress_matrix(values):
    return jnp.stack(
        [
            jnp.stack([values[0], values[3], values[4]]),
            jnp.stack([values[3], values[1], values[5]]),
            jnp.stack([values[4], values[5], values[2]]),
        ]
    )


def body(wave_coeffs, projectors, miller_index, lattice, occupation, species, proj_count, coupling):
    weights = cart_weights(miller_index, lattice)
    band_count = wave_coeffs.shape[1]
    group_slot = lax.axis_index(GVEC)
    atom_total = species.shape[0]
    flat_waves = wave_coeffs.reshape(2 * band_count, wave_coeffs.shape[2])
    total_proj = PROJ * lax.axis_size(BAND)
    start_carry = jnp.zeros((band_count, 10, 2, total_proj), jnp.float32)
    arrived = lax.all_gather(projectors, BAND, axis=1, tiled=True)
    block_rows = arrived.shape[1]
    anchor = jnp.zeros((), jnp.int32)

    def one_atom(atom_slot, partial_value):
        atom_block = lax.dynamic_slice_in_dim(arrived, atom_slot * PROJ, PROJ, 1)
        values = intersection(scale_block(weights, atom_block), flat_waves).transpose(3, 0, 1, 2)
        return lax.dynamic_update_slice(
            partial_value, values, (anchor, anchor, anchor, atom_slot * PROJ)
        )

    intersections = lax.fori_loop(0, block_rows // PROJ, one_atom, start_carry)
    couplings = atom_couplings(species, proj_count, coupling)
    owned_atoms_rows = sent_and_summed(intersections.astype(jnp.bfloat16), GVEC, 3)
    atom_quarter = atom_total // lax.axis_size(GVEC)
    per_atom = owned_atoms_rows.reshape(band_count, 10, 2, atom_quarter, PROJ).transpose(
        1, 2, 3, 4, 0
    )
    local_couplings = lax.dynamic_slice_in_dim(
        couplings, group_slot * atom_quarter, atom_quarter, 0
    )
    quarter_force, stress_part = contract(per_atom, local_couplings, occupation)
    anchor = jnp.zeros((), jnp.int32)
    force_part = lax.dynamic_update_slice(
        jnp.zeros((3, atom_total), jnp.float32), quarter_force, (anchor, group_slot * atom_quarter)
    )
    band_total = band_count * lax.axis_size(BAND)
    force_scale = 2.0 / (PROJ * math.sqrt(band_total))
    stress_scale = 1.0 / (PROJ * math.sqrt(atom_total * band_total))
    across = taken_together(force_part, GVEC)
    own_force = sum_at_owner(across, BAND, 1)
    total_stress = one_axis_at_a_time(stress_part, BAND_GVEC)
    return (own_force * force_scale, stress_matrix(total_stress * stress_scale))


def solution(mesh):
    finer = Mesh(
        mesh.devices.reshape(4, 2, 4, 2, 2), ("band_0", "band_1", "band_2", "gvec_0", "gvec_1")
    )
    in_specs = (
        P(None, BAND, GVEC),
        P(None, BAND, GVEC),
        P(None, GVEC),
        P(),
        P(BAND),
        P(),
        P(),
        P(),
    )
    out_specs = (P(None, BAND), P())
    return jax.shard_map(body, mesh=finer, in_specs=in_specs, out_specs=out_specs, check_vma=False)
```

profile of v0, /device:TPU:1, one launch (start us, length us, event | category | flops | bytes accessed | tf_op | source)
XLA Modules:
  0.0 410.5 jit_solution(7296648084698257175)
XLA Ops:
  11.4 4.1 %fusion.27 = (f32[1,18816]{1,0:T(1,128)S(1)}, f32[1,18816]{1,0:T(1,128)S(1)}, f32[1,18816]{1,0:T(1,128)S(1)}) fusion(f32[]{:T(128)} %bitcast.16, f32[3,18816]{1,0:T(4,128)S(1)} %convert_element_type.38, f32[]{:T(128)} %bitcast.15, f32[]{:T(128)} %bitcast.14, f32[]{:T(128)} %bitcast.13, f32[]{:T(128)} %bitcast.12, f32[]{:T(128)} %bitcast.11), kind=kLoop, calls=%fused_computation.59 | loop fusion | flops 244608 | bytes 451608 | tf_op jit(solution)/shard_map/mul | solution.py:69
  19.6 163.9 %all-gather.2.cloned.1.call-done = bf16[2,256,18816]{2,1,0:T(8,128)(2,1)} async-done(((bf16[2,8,18816]{2,1,0:T(8,128)(2,1)}), bf16[2,256,18816]{2,1,0:T(8,128)(2,1)}) %all-gather.2.cloned.1.call-update) | async-done | bytes 19267600 | tf_op jit(solution)/shard_map/all_gather | solution.py:134
  183.8 149.6 %while.13 = (s32[]{:T(128)}, bf16[32,10,2,256]{0,3,1,2:T(8,128)(2,1)S(1)}, f32[10,18816]{1,0:T(8,128)S(1)}, bf16[2,256,18816]{2,1,0:T(8,128)(2,1)}, bf16[64,1881...) while((s32[]{:T(128)}, bf16[32,10,2,256]{0,3,1,2:T(8,128)(2,1)S(1)}, ...), condition=%wide.region_1.0_spmd, body=%wide.region_0.0_spmd.sunk | while | flops 391704576 | bytes 6345875 | solution.py:145
  184.9 3.4 fusion.42
  194.3 3.4 fusion.42
  199.0 3.4 fusion.42
  208.3 3.4 fusion.42
  213.0 3.4 fusion.42
  217.7 3.4 fusion.42
  227.0 3.4 fusion.42
  236.4 3.4 fusion.42
  245.7 3.4 fusion.42
  255.1 3.4 fusion.42
  259.7 3.4 fusion.42
  264.4 3.4 fusion.42
  273.7 3.4 fusion.42
  283.1 3.4 fusion.42
  292.4 3.4 fusion.42
  301.8 3.4 fusion.42
  311.1 3.4 fusion.42
  320.5 3.4 fusion.42
  329.8 3.4 fusion.42
  335.4 4.8 %all-to-all-start = ((bf16[4,2,20480]{2,1,0:T(2,128)(2,1)}), bf16[4,2,20480]{2,1,0:T(2,128)(2,1)S(1)}, u32[]{:S(2)}, u32[]{:S(2)}) async-start(bf16[4,2,20480]{2,1,0:T(2,128)(2,1)} %reshape.141), calls=%async_computation | async-start | bytes 655360 | tf_op jit(solution)/shard_map/all_to_all | solution.py:26
  340.3 5.7 %all-to-all-done = bf16[4,2,20480]{2,1,0:T(2,128)(2,1)S(1)} async-done(((bf16[4,2,20480]{2,1,0:T(2,128)(2,1)}), bf16[4,2,20480]{2,1,0:T(2,128)(2,1)S(1)}, u32[]{:S(2)}, u32[]{:S(2)}) %all-to-all-start) | async-done | bytes 327712 | tf_op jit(solution)/shard_map/all_to_all | solution.py:26
  348.0 8.4 %psum.35 = f32[6]{0:T(128)S(1)} all-reduce(f32[6]{0:T(128)S(1)} %multiply_reduce_fusion), channel_id=1, replica_groups=mesh['band_0'=4,'band_1'=2,'band_2'=4,'gvec_0'=2,'gvec_1'=2] {'band_0'}, use_global_device_ids=true, to_apply=%region_9.0 | all-reduce | flops 6 | bytes 48 | tf_op jit(solution)/shard_map/psum | solution.py:50
  356.4 5.3 %psum.36 = f32[6]{0:T(128)S(1)} all-reduce(f32[6]{0:T(128)S(1)} %psum.35), channel_id=1, replica_groups=mesh['band_0'=4,'band_1'=2,'band_2'=4,'gvec_0'=2,'gvec_1'=2] {'band_1'}, use_global_device_ids=true, to_apply=%region_10.0 | all-reduce | flops 6 | bytes 48 | tf_op jit(solution)/shard_map/psum | solution.py:50
  361.6 6.7 %psum.37 = f32[6]{0:T(128)S(1)} all-reduce(f32[6]{0:T(128)S(1)} %psum.36), channel_id=1, replica_groups=mesh['band_0'=4,'band_1'=2,'band_2'=4,'gvec_0'=2,'gvec_1'=2] {'band_2'}, use_global_device_ids=true, to_apply=%region_11.0 | all-reduce | flops 6 | bytes 48 | tf_op jit(solution)/shard_map/psum | solution.py:50
  368.3 3.8 psum.38
  372.1 9.3 %psum.39 = f32[6]{0:T(128)S(1)} all-reduce(f32[6]{0:T(128)S(1)} %psum.38), channel_id=1, replica_groups=mesh['band_0'=4,'band_1'=2,'band_2'=4,'gvec_0'=2,'gvec_1'=2] {'gvec_1'}, use_global_device_ids=true, to_apply=%region_13.0 | all-reduce | flops 6 | bytes 48 | tf_op jit(solution)/shard_map/psum | solution.py:50
  383.1 3.4 all-to-all-start.1
  390.5 3.9 all-to-all-start.2
  395.0 8.1 %all-to-all-done.2 = f32[32,3,1]{1,2,0:T(1,128)S(1)} async-done(((f32[32,3,1]{1,2,0:T(1,128)}), f32[32,3,1]{1,2,0:T(1,128)S(1)}, u32[]{:S(2)}, u32[]{:S(2)}) %all-to-all-start.2) | async-done | bytes 416 | tf_op jit(solution)/shard_map/all_to_all | solution.py:44
  (191 shorter events, 102.3 us)
Async XLA Ops:
  7.2 12.2 %copy-start = (f32[4,8,8]{2,1,0:T(8,128)S(1)}, f32[4,8,8]{2,1,0:T(8,128)}, u32[]{:S(2)}) copy-start(f32[4,8,8]{2,1,0:T(8,128)} %param.17) | copy-start | bytes 3076
  7.2 176.3 %all-gather.2.cloned.1.call-start = ((), (), s32[]{:S(2)}) async-start(), calls=%async_computation.3 | async-start | bytes 19869696 | tf_op jit(solution)/shard_map/all_gather | solution.py:134
  17.8 1.6 copy-start.2
  335.4 10.6 %all-to-all-start = ((bf16[4,2,20480]{2,1,0:T(2,128)(2,1)}), bf16[4,2,20480]{2,1,0:T(2,128)(2,1)S(1)}, u32[]{:S(2)}, u32[]{:S(2)}) async-start(bf16[4,2,20480]{2,1,0:T(2,128)(2,1)} %reshape.141), calls=%async_computation | async-start | bytes 655360 | tf_op jit(solution)/shard_map/all_to_all | solution.py:26
  346.8 1.0 copy-start.1
  383.1 6.7 %all-to-all-start.1 = ((f32[4,3,32]{2,1,0:T(4,128)}), f32[4,3,32]{2,1,0:T(4,128)S(1)}, u32[]{:S(2)}, u32[]{:S(2)}) async-start(f32[4,3,32]{2,1,0:T(4,128)} %broadcast_in_dim.14), calls=%async_computation.1 | async-start | bytes 16384 | tf_op jit(solution)/shard_map/all_to_all | solution.py:32
  390.5 12.5 %all-to-all-start.2 = ((f32[32,3,1]{1,2,0:T(1,128)}), f32[32,3,1]{1,2,0:T(1,128)S(1)}, u32[]{:S(2)}, u32[]{:S(2)}) async-start(f32[32,3,1]{1,2,0:T(1,128)} %copy.99), calls=%async_computation.2 | async-start | bytes 32768 | tf_op jit(solution)/shard_map/all_to_all | solution.py:44
Sparse Core Ops, SparseCore 0:
  11.0 172.4 all-gather.1
where the time goes:
time: 414 us; the launch traced here: 410 us
  waiting for transfers between devices  178 us (43%)
  matrix products  110 us (27%)
  other arithmetic  51.5 us (12%)
  blocking collectives  33.4 us (8%)
  between operations  14.2 us (3%)
  starting transfers between devices  12.2 us (3%)
  local copies, waits for them, and re-layouts  8.72 us (2%)
    all_gather x1, waiting for transfers between devices, body(): arrived = lax.all_gather(projectors, BAND, axis=1, tiled=True)  164 us
    dot_general x32, matrix products, intersection(): lax.dot_general(scaled, flat_waves, (((1,), (1,)), ((), ())), preferred_e...  110 us
    convert_element_type x32, other arithmetic, scale_block(): atom_block[None].astype(jnp.float32)  36.9 us
    psum x5, blocking collectives, one_axis_at_a_time(): array = lax.psum(array, axis)  33.4 us
  transfers between devices with their start and end apart: 4, of which 3 were waited for; matrix products, arithmetic and copies ran while one was open for 4% of the time, Pallas kernels for 0%

commit v1 on v0

v1 whole, which is shorter than its diff:
```python
import functools
import math

import jax
import jax.numpy as jnp
from jax import lax
from jax.experimental import pallas as pl
from jax.experimental.pallas import tpu as pltpu
from jax.sharding import Mesh
from jax.sharding import PartitionSpec as P

PROJ = 8
MILLER = 24.0
LANE = 128
MESH = pl.DeviceIdType.MESH
F32 = jnp.float32
BF16 = jnp.bfloat16
AXES = ("z", "yh", "x", "yl", "core")


def kernel(
    dims, nt, tiles, chunks, scales,
    psi_hbm, proj_hbm, miller_hbm, lat_ref, occ_ref, spec_ref, cnt_ref, coup_ref,
    force_ref, stress_ref,
    psi_buf, p_buf, mil_buf, occ_buf, w_buf, acc, b_send, rs_buf, uv_buf, negv, facc, sacc, tot_a, tot_b,
    loc_sem, psend, precv, zsend, zrecv, ssend, srecv, osend, orecv, rsend, rrecv, asend, arecv, fsend, frecv, gsend, grecv,
):
    nz, nyh, nx, nyl, nc = dims
    n_s = nyh * nx
    n_r = n_s * nyl * nc
    z, yh, x, yl, c = (lax.axis_index(a) for a in AXES)
    me_s = yh * nx + x
    me_r = me_s * (nyl * nc) + yl * nc + c
    beta = z * n_s + me_s
    n_chunk = len(chunks)

    def s_peer(k):
        q = lax.rem(me_s + k, n_s)
        return q, {"yh": q // nx, "x": lax.rem(q, nx)}

    def r_peer(k):
        r = lax.rem(me_r + k, n_r)
        q = r // (nyl * nc)
        rest = lax.rem(r, nyl * nc)
        return r, {"yh": q // nx, "x": lax.rem(q, nx), "yl": rest // nc, "core": lax.rem(rest, nc)}

    def z_peer(k):
        return {"z": lax.rem(z + k, nz)}

    def first_tile(q):
        return (q * tiles) // n_s

    def remote(src, dst, ssem, rsem, where):
        return pltpu.make_async_remote_copy(src, dst, ssem, rsem, device_id=where, device_id_type=MESH)

    def wait_recv(ref, sem):
        remote(ref, ref, sem, sem, s_peer(1)[1]).wait_recv()

    def wait_send(ref, sem):
        remote(ref, ref, sem, sem, s_peer(1)[1]).wait_send()

    my_off = first_tile(me_s) * LANE

    def local_copies():
        out = [pltpu.make_async_copy(miller_hbm.at[:, pl.ds(pl.multiple_of(my_off, LANE), nt * LANE)], mil_buf.at[:, pl.ds(0, nt * LANE)], loc_sem.at[0])]
        out.append(pltpu.make_async_copy(
            proj_hbm.at[:, :, pl.ds(pl.multiple_of(my_off, LANE), nt * LANE)],
            p_buf.at[:, beta, :, pl.ds(0, nt * LANE)], loc_sem.at[1]))
        out.append(pltpu.make_async_copy(
            psi_hbm.at[:, :, pl.ds(pl.multiple_of(my_off, LANE), nt * LANE)],
            psi_buf.at[:, pl.ds(pl.multiple_of(me_s * 32, 32), 32), pl.ds(0, nt * LANE)], loc_sem.at[2]))
        return out

    for cp in local_copies():
        cp.start()

    bar = pltpu.get_barrier_semaphore()

    def hello(k, carry):
        _, where = r_peer(k)
        pl.semaphore_signal(bar, 1, device_id=where, device_id_type=MESH)
        return carry

    lax.fori_loop(1, n_r, hello, 0)
    for k in range(1, nz):
        pl.semaphore_signal(bar, 1, device_id=z_peer(k), device_id_type=MESH)
    pl.semaphore_wait(bar, n_r - 1 + nz - 1)

    for i, (t0, tn) in enumerate(chunks):
        for k in range(1, n_s):
            q, where = s_peer(k)
            off = pl.multiple_of((first_tile(q) + t0) * LANE, LANE)
            remote(proj_hbm.at[:, :, pl.ds(off, tn * LANE)],
                   p_buf.at[:, beta, :, pl.ds(t0 * LANE, tn * LANE)], psend, precv.at[i], where).start()
    for k in range(1, n_s):
        q, where = s_peer(k)
        remote(occ_ref, occ_buf.at[me_s], osend, orecv, where).start()
    for i, (t0, tn) in enumerate(chunks):
        for k in range(1, n_s):
            q, where = s_peer(k)
            off = pl.multiple_of((first_tile(q) + t0) * LANE, LANE)
            remote(psi_hbm.at[:, :, pl.ds(off, tn * LANE)],
                   psi_buf.at[:, pl.ds(pl.multiple_of(me_s * 32, 32), 32), pl.ds(t0 * LANE, tn * LANE)], ssend, srecv.at[i], where).start()

    local = local_copies()
    local[0].wait()
    kp = w_buf.shape[1]
    used = nt * LANE
    if kp > used:
        pad = kp - used
        mil_buf[:, pl.ds(used, pad)] = jnp.zeros((3, pad), jnp.int32)
        psi_buf[:, :, pl.ds(used, pad)] = jnp.zeros((2, psi_buf.shape[1], pad), BF16)
        p_buf[:, :, :, pl.ds(used, pad)] = jnp.zeros((2, p_buf.shape[1], PROJ, pad), BF16)
    own_tiles = first_tile(me_s + 1) - first_tile(me_s)
    valid = (lax.broadcasted_iota(jnp.int32, (1, kp), 1) < own_tiles * LANE).astype(F32)
    idx = [mil_buf[a : a + 1, :].astype(F32) for a in range(3)]
    co = [(idx[0] * lat_ref[0, a] + idx[1] * lat_ref[1, a] + idx[2] * lat_ref[2, a]) / MILLER for a in range(3)]
    iso = (co[0] * co[0] + co[1] * co[1] + co[2] * co[2]) / 3.0
    rows = list(co)
    for a, b in ((0, 0), (1, 1), (2, 2), (0, 1), (0, 2), (1, 2)):
        prod = co[a] * co[b]
        rows.append(prod - iso if a == b else prod)
    for m, row in enumerate(rows):
        w_buf[m : m + 1, :] = row * valid
    facc[...] = jnp.zeros_like(facc)
    sacc[...] = jnp.zeros_like(sacc)
    acc[...] = jnp.zeros_like(acc)

    local[1].wait()
    plane = pl.ds(pl.multiple_of(z * n_s, n_s), n_s)
    for i, (t0, tn) in enumerate(chunks):
        part = pl.ds(t0 * LANE, tn * LANE)
        wait_recv(p_buf.at[:, pl.ds(0, n_s - 1), :, part], precv.at[i])
        for k in range(1, nz):
            remote(p_buf.at[:, plane, :, part], p_buf.at[:, plane, :, part], zsend, zrecv.at[i], z_peer(k)).start()

    local[2].wait()
    nb = psi_buf.shape[1]
    na = p_buf.shape[1]
    for i, (t0, tn) in enumerate(chunks):
        part = pl.ds(t0 * LANE, tn * LANE)
        wait_recv(p_buf.at[:, pl.ds(0, n_s * (nz - 1)), :, part], zrecv.at[i])
        wait_recv(psi_buf.at[:, pl.ds(0, 32 * (n_s - 1)), part], srecv.at[i])
        rhs = psi_buf[:, :, part].reshape(2 * nb, tn * LANE)
        lhs = p_buf[:, :, :, part].reshape(2 * na * PROJ, tn * LANE)
        if i == n_chunk - 1:
            keep = (lax.broadcasted_iota(jnp.int32, (1, tn * LANE), 1) + t0 * LANE < own_tiles * LANE)
            lhs = jnp.where(keep, lhs, jnp.zeros_like(lhs))
        acc[...] += lax.dot_general(lhs, rhs, (((1,), (1,)), ((), ())), preferred_element_type=F32)

    np_ = na * PROJ
    b_send[:, 0] = (acc[:np_, :nb] + acc[np_:, nb:]).reshape(na, PROJ, nb).astype(BF16)
    b_send[:, 1] = (acc[:np_, nb:] - acc[np_:, :nb]).reshape(na, PROJ, nb).astype(BF16)

    def give(k, carry):
        r, where = r_peer(k)
        remote(b_send.at[r], rs_buf.at[me_r], rsend, rrecv, where).start()
        return carry

    lax.fori_loop(1, n_r, give, 0)
    rs_buf[me_r] = b_send[me_r]
    wait_recv(occ_buf.at[pl.ds(0, n_s - 1)], orecv)
    occ_buf[me_s] = occ_ref[...]
    occ = jnp.sum(occ_buf[...], axis=0)
    kind = spec_ref[me_r]
    count = cnt_ref[me_r]
    mat = coup_ref[kind]
    act = (lax.broadcasted_iota(jnp.int32, (PROJ, PROJ), 0) < count) & (lax.broadcasted_iota(jnp.int32, (PROJ, PROJ), 1) < count)
    mat = jnp.where(act, mat, 0.0)
    wait_recv(rs_buf.at[pl.ds(0, n_r - 1)], rrecv)
    total = jnp.sum(rs_buf[...].astype(F32), axis=0)
    for h in range(2):
        mixed = jnp.zeros((PROJ, nb), F32)
        for i in range(PROJ):
            mixed = mixed + mat[:, i : i + 1] * total[h, i : i + 1, :]
        uv_buf[h, me_r] = (mixed * occ).astype(BF16)

    def spread(k, carry):
        _, where = r_peer(k)
        remote(uv_buf.at[:, me_r], uv_buf.at[:, me_r], asend, arecv, where).start()
        return carry

    lax.fori_loop(1, n_r, spread, 0)
    wait_recv(uv_buf.at[:, pl.ds(0, n_r - 1)], arecv)

    u = uv_buf[0].reshape(np_, nb)
    v = uv_buf[1].reshape(np_, nb)
    negv[0] = u
    negv[1] = v
    negv[2] = -v

    wide = 256

    def block(i, carry):
        cols = pl.ds(pl.multiple_of(i * wide, wide), wide)
        re = psi_buf[0, :, cols]
        im = psi_buf[1, :, cols]
        dot = functools.partial(jnp.dot, preferred_element_type=F32)
        y_re = dot(negv[0], re) + dot(negv[1], im)
        y_im = dot(negv[0], im) + dot(negv[2], re)
        p_re = p_buf[0, :, :, cols].astype(F32).reshape(np_, wide)
        p_im = p_buf[1, :, :, cols].astype(F32).reshape(np_, wide)
        e_im = (p_re * y_im - p_im * y_re).reshape(na, PROJ, wide)
        e_re = jnp.sum((p_re * y_re + p_im * y_im).reshape(na, PROJ, wide), axis=0)
        for a in range(3):
            t = e_im * w_buf[a : a + 1, cols].reshape(1, 1, wide)
            facc[a] += t[:, :, :LANE] + t[:, :, LANE:]
        for m in range(6):
            t = e_re * w_buf[3 + m : 4 + m, cols]
            sacc[m] += t[:, :LANE] + t[:, LANE:]
        return carry

    lax.fori_loop(0, kp // wide, block, 0)

    out_rows = []
    for a in range(3):
        f = jnp.sum(facc[a], axis=1)
        if na < LANE:
            f = jnp.concatenate([f, jnp.zeros((LANE - na, LANE), F32)], axis=0)
        out_rows.append(jnp.sum(f.T, axis=0, keepdims=True))
    lane = lax.broadcasted_iota(jnp.int32, (1, LANE), 1)
    srow = jnp.zeros((1, LANE), F32)
    for m in range(6):
        srow = srow + jnp.where(lane == m, jnp.sum(sacc[m], keepdims=True), 0.0)
    mine = jnp.concatenate(out_rows + [srow] + [jnp.zeros((4, LANE), F32)], axis=0)
    tot_a[me_r] = mine

    def share(k, carry):
        _, where = r_peer(k)
        remote(tot_a.at[me_r], tot_a.at[me_r], fsend, frecv, where).start()
        return carry

    lax.fori_loop(1, n_r, share, 0)
    wait_recv(tot_a.at[pl.ds(0, n_r - 1)], frecv)
    tot_b[z] = jnp.sum(tot_a[...], axis=0)
    for k in range(1, nz):
        remote(tot_b.at[z], tot_b.at[z], gsend, grecv, z_peer(k)).start()
    wait_recv(tot_b.at[pl.ds(0, nz - 1)], grecv)
    res = jnp.sum(tot_b[...], axis=0)
    force_ref[...] = jnp.sum(jnp.where(lane == beta, res[0:3, :], 0.0), axis=1, keepdims=True) * scales[0]
    i0 = lax.broadcasted_iota(jnp.int32, (3, 3), 0)
    i1 = lax.broadcasted_iota(jnp.int32, (3, 3), 1)
    st = jnp.zeros((3, 3), F32)
    for m, (a, b) in enumerate(((0, 0), (1, 1), (2, 2), (0, 1), (0, 2), (1, 2))):
        val = jnp.sum(jnp.where(lane == m, res[3:4, :], 0.0), axis=1, keepdims=True)
        hit = ((i0 == a) & (i1 == b)) | ((i0 == b) & (i1 == a))
        st = st + jnp.where(hit, val, 0.0)
    stress_ref[...] = st * scales[1]

    for i, (t0, tn) in enumerate(chunks):
        part = pl.ds(t0 * LANE, tn * LANE)
        wait_send(p_buf.at[:, pl.ds(0, n_s - 1), :, part], psend)
        wait_send(psi_buf.at[:, pl.ds(0, 32 * (n_s - 1)), part], ssend)
        wait_send(p_buf.at[:, pl.ds(0, n_s * (nz - 1)), :, part], zsend)
    wait_send(occ_buf.at[pl.ds(0, n_s - 1)], osend)
    wait_send(rs_buf.at[pl.ds(0, n_r - 1)], rsend)
    wait_send(uv_buf.at[:, pl.ds(0, n_r - 1)], asend)
    wait_send(tot_a.at[pl.ds(0, n_r - 1)], fsend)
    wait_send(tot_b.at[pl.ds(0, nz - 1)], gsend)


def body(dims, psi, proj, miller, lattice, occupation, species, proj_count, coupling):
    nz, nyh, nx, nyl, nc = dims
    n_s = nyh * nx
    n_r = n_s * nyl * nc
    bands = psi.shape[1]
    tiles = psi.shape[2] // LANE
    atoms = species.shape[0]
    nt = -(-tiles // n_s)
    sizes = []
    left = nt
    for want in (6, 6, 4):
        if left > want:
            sizes.append(want)
            left -= want
    sizes.append(left)
    chunks, at = [], 0
    for n in sizes:
        chunks.append((at, n))
        at += n
    kp = -(-nt * LANE // 256) * 256
    nb = n_s * bands
    me_s = lax.axis_index("yh") * nx + lax.axis_index("x")
    zero = jnp.zeros((), jnp.int32)
    occ_row = lax.dynamic_update_slice(jnp.zeros((1, nb), F32), occupation[None], (zero, me_s * bands))
    band_total = nb * nz
    scales = (2.0 / (PROJ * math.sqrt(band_total)), 1.0 / (PROJ * math.sqrt(atoms * band_total)))
    any_spec = pl.BlockSpec(memory_space=pl.ANY)
    vmem = pl.BlockSpec(memory_space=pltpu.VMEM)
    smem = pl.BlockSpec(memory_space=pltpu.SMEM)
    dma = pltpu.SemaphoreType.DMA
    nch = len(chunks)
    return pl.pallas_call(
        functools.partial(kernel, dims, nt, tiles, tuple(chunks), scales),
        out_shape=(jax.ShapeDtypeStruct((3, 1), F32), jax.ShapeDtypeStruct((3, 3), F32)),
        in_specs=[any_spec, any_spec, any_spec, smem, vmem, smem, smem, vmem],
        out_specs=(vmem, vmem),
        scratch_shapes=[
            pltpu.VMEM((2, nb, kp), BF16),
            pltpu.VMEM((2, atoms, PROJ, kp), BF16),
            pltpu.VMEM((3, kp), jnp.int32),
            pltpu.VMEM((n_s, 1, nb), F32),
            pltpu.VMEM((16, kp), F32),
            pltpu.VMEM((2 * atoms * PROJ, 2 * nb), F32),
            pltpu.VMEM((atoms, 2, PROJ, nb), BF16),
            pltpu.VMEM((n_r, 2, PROJ, nb), BF16),
            pltpu.VMEM((2, n_r, PROJ, nb), BF16),
            pltpu.VMEM((3, atoms * PROJ, nb), BF16),
            pltpu.VMEM((3, atoms, PROJ, LANE), F32),
            pltpu.VMEM((6, PROJ, LANE), F32),
            pltpu.VMEM((n_r, 8, LANE), F32),
            pltpu.VMEM((nz, 8, LANE), F32),
            dma((3,)), dma, dma((nch,)), dma, dma((nch,)), dma, dma((nch,)), dma, dma, dma, dma, dma, dma, dma, dma, dma, dma,
        ],
        compiler_params=pltpu.CompilerParams(collective_id=0, has_side_effects=True, vmem_limit_bytes=58 << 20),
        name="plane_kernel",
    )(psi, proj, miller, lattice, occ_row, species, proj_count, coupling)


def solution(mesh, dims=(4, 2, 4, 2, 2)):
    finer = Mesh(mesh.devices.reshape(dims), AXES)
    band, gvec = ("z", "yh", "x"), ("yl", "core")
    in_specs = (P(None, band, gvec), P(None, band, gvec), P(None, gvec), P(), P(band), P(), P(), P())
    return jax.shard_map(functools.partial(body, dims), mesh=finer, in_specs=in_specs, out_specs=(P(None, band), P()), check_vma=False)
```

time: 414 us -> 78.4 us (0.19)
  waiting for transfers between devices: 178 us -> 0 us
  matrix products: 110 us -> 0 us
  Pallas kernels: 0 us -> 73.7 us
  other arithmetic: 51.5 us -> 0 us
  blocking collectives: 33.4 us -> 0 us
  between operations: 14.2 us -> 0.65 us
  starting transfers between devices: 12.2 us -> 0 us
  local copies, waits for them, and re-layouts: 8.72 us -> 3.83 us
    all_gather x1 -> x0, waiting for transfers between devices: 164 us -> none  [body(): arrived = lax.all_gather(projectors, BAND, axis=1, tiled=True)]
    dot_general x34 -> x0, matrix products: 110 us -> none  [the longest x32 110 us: intersection(): lax.dot_general(scaled, flat_waves, (((1,), (1,)), ((), ())), preferred_e...]
    pallas_call x0 -> x1, Pallas kernels: none -> 73.7 us  [body(): pl.pallas_call(functools.partial(kernel, dims, nt, tiles, tuple(chunks),...]
    convert_element_type x34 -> x0, other arithmetic: 38.6 us -> none  [the longest x32 36.9 us: scale_block(): atom_block[None].astype(jnp.float32)]
    psum x5 -> x0, blocking collectives: 33.4 us -> none  [one_axis_at_a_time(): array = lax.psum(array, axis)]
    all_to_all x3 -> x0, waiting for transfers between devices: 13.7 us -> none  [the longest x1 8.08 us: sum_at_owner(): parts = lax.all_to_all(split_up(array, dim, count), axis, 0, 0, tiled=True)]
    all_to_all x3 -> x0, starting transfers between devices: 12.1 us -> none  [the longest x1 4.82 us: sent_and_summed(): parts = lax.all_to_all(split_up(array, dim, count), axis, 0, 0, tiled=True)]
    mul x4 -> x0, other arithmetic: 6.74 us -> none  [the longest x2 6.22 us: cart_weights(): product = coords[first_axis] * coords[second_axis]]
  transfers between devices with their start and end apart: 4 -> 0, of which waited for: 3 -> 0; matrix products, arithmetic and copies ran while one was open for 4% -> 0% of each run, Pallas kernels for 0% -> 0%
where the time goes in v1:
time: 78.4 us; the launch traced here: 78.2 us
  Pallas kernels  73.7 us (94%)
  local copies, waits for them, and re-layouts  3.83 us (5%)
    pallas_call x1, Pallas kernels, body(): pl.pallas_call(functools.partial(kernel, dims, nt, tiles, tuple(chunks),...  73.7 us
    unnamed x3, local copies, waits for them, and re-layouts  1.81 us

profile of v1, /device:TPU:1, one launch (start us, length us, event | category | flops | bytes accessed | tf_op | source)
XLA Modules:
  0.0 78.2 jit_solution(14855204992538515287)
XLA Ops:
  0.6 0.8 dynamic_update_slice.3.occ_ref
  1.4 0.0 copy-start
  1.4 0.6 copy-done
  2.0 73.7 %plane_kernel.1 = (f32[3,1]{1,0:T(4,128)}, f32[3,3]{1,0:T(4,128)}) custom-call(bf16[2,32,18816]{2,1,0:T(8,128)(2,1)} %psi_hbm.1, bf16[2,8,18816]{2,1,0:T(8,128)(2,1)} %proj_hbm.1, s32[3,18816]{1,0:T(4,128)} %miller_hbm.1, f32[3,3]{1,0:T(4,128)} %lat_ref.1, f32[1,256]{1,0:T(1,128)} %copy-done, s32[32]{0:T(128)} %spec_ref.1, s32[32]{0:T(128)} %cnt_ref.1, ...), custom_call_target="tpu_custom_call" | custom-call | tf_op jit(solution)/shard_map/plane_kernel/pallas_call | solution.py:293
  75.7 1.2 %copy.10 = f32[3,1]{0,1:T(1,128)} copy(f32[3,1]{1,0:T(4,128)} %get-tuple-element.2) | data formatting | bytes 24 | tf_op jit(solution)/shard_map/plane_kernel/pallas_call | solution.py:293
  76.9 1.2 %copy.13 = f32[3,3]{1,0:T(4,128)} copy(f32[3,3]{1,0:T(4,128)} %get-tuple-element.7) | data formatting | bytes 72
  (1 shorter events, 0.0 us)
Async XLA Ops:
  1.4 0.6 copy-start

commit v2 on v1

v2 whole, which is shorter than its diff:
```python
import functools
import itertools
import math

import jax
import jax.numpy as jnp
from jax import lax
from jax.experimental import pallas as pl
from jax.experimental.pallas import tpu as pltpu
from jax.sharding import Mesh
from jax.sharding import PartitionSpec as P

PROJ = 8
MILLER = 24.0
LANE = 128
LOGICAL = pl.DeviceIdType.LOGICAL
F32 = jnp.float32
BF16 = jnp.bfloat16
AXES = ("z", "yh", "x", "yl", "core")


def kernel(
    dims, nt, tiles, chunks,
    psi_hbm, proj_hbm, miller_hbm, lat_hbm, occ_hbm, spec_hbm, cnt_hbm, coup_hbm,
    out_ref,
    psi_buf, p_buf, mil_buf, occ_buf, w_buf, acc, b_send, rs_buf, uv_buf, negv, facc, sacc, tot,
    lat_ref, spec_ref, cnt_ref, coup_ref, occ_row, occ_in,
    loc_sem, psend, precv, zsend, zrecv, ssend, srecv, osend, orecv, rsend, rrecv, asend, arecv, fsend, frecv,
):
    nz, nyh, nx, nyl, nc = dims
    n_s = nyh * nx
    n_r = n_s * nyl * nc
    z, yh, x, yl, c = (lax.axis_index(a) for a in AXES)
    me_s = yh * nx + x
    me_r = me_s * (nyl * nc) + yl * nc + c
    beta = z * n_s + me_s
    n_chunk = len(chunks)

    n_all = nz * n_r
    me = z * n_r + me_r

    strides = (n_r, nx * nyl * nc, nyl * nc, nc, 1)
    digits = []
    for at, n, stride in zip((z, yh, x, yl, c), dims, strides):
        digits.append([jnp.where(at + k >= n, at + k - n, at + k) * stride if k else at * stride for k in range(n)])

    def hops(offset):
        dz, a, b, d, e = offset
        return min(dz, nz - dz) + min(b, nx - b) + (2 if a and not d else 1 if a or d else 0)

    def peers(free):
        spans = [range(n) if f else (0,) for n, f in zip(dims, free)]
        offsets = [o for o in itertools.product(*spans) if any(o)]
        return sorted(offsets, key=lambda o: -hops(o))

    def number(offset):
        return sum(digits[i][k] for i, k in enumerate(offset))

    s_peers = peers((0, 1, 1, 0, 0))
    r_peers = peers((0, 1, 1, 1, 1))
    z_peers = peers((1, 0, 0, 0, 0))
    all_peers = peers((1, 1, 1, 1, 1))
    base = digits[0][0]

    def slice_of(offset):
        return (digits[1][offset[1]] + digits[2][offset[2]]) // (nyl * nc)

    def first_tile(q):
        return (q * tiles) // n_s

    def remote(src, dst, ssem, rsem, where):
        return pltpu.make_async_remote_copy(src, dst, ssem, rsem, device_id=where, device_id_type=LOGICAL)

    def wait_recv(ref, sem):
        remote(ref, ref, sem, sem, number(s_peers[0])).wait_recv()

    def wait_send(ref, sem):
        remote(ref, ref, sem, sem, number(s_peers[0])).wait_send()

    my_off = pl.multiple_of(first_tile(me_s) * LANE, LANE)

    def extra(q):
        return first_tile(q + 1) - first_tile(q) > nt

    if_extra = pl.when(extra(me_s))
    last = pl.ds(nt * LANE, LANE)

    own_rows = pl.ds(pl.multiple_of(me_s * 32, 32), 32)

    def local_copies(t0, tn):
        here = pl.ds(pl.multiple_of(my_off + t0 * LANE, LANE), tn * LANE)
        there = pl.ds(t0 * LANE, tn * LANE)
        return [pltpu.make_async_copy(miller_hbm.at[:, here], mil_buf.at[:, there], loc_sem.at[0]),
                pltpu.make_async_copy(proj_hbm.at[:, :, here], p_buf.at[:, beta, :, there], loc_sem.at[1]),
                pltpu.make_async_copy(psi_hbm.at[:, :, here], psi_buf.at[:, own_rows, there], loc_sem.at[2])]

    small = [pltpu.make_async_copy(a, b, loc_sem.at[3 + n]) for n, (a, b) in enumerate((
        (occ_hbm, occ_in), (lat_hbm, lat_ref), (spec_hbm, spec_ref), (cnt_hbm, cnt_ref), (coup_hbm, coup_ref)))]

    bar = pltpu.get_barrier_semaphore()
    for o in sorted(z_peers + r_peers, key=lambda o: -hops(o)):
        pl.semaphore_signal(bar, 1, device_id=number(o), device_id_type=LOGICAL)
    occ_row[...] = jnp.zeros_like(occ_row)
    for cp in small + local_copies(0, nt):
        cp.start()

    @if_extra
    def _():
        for cp in local_copies(nt, 1):
            cp.start()

    pl.semaphore_wait(bar, n_r - 1 + nz - 1)

    def send_slices(src, dst_of, ssem, rsem):
        for i, (t0, tn) in enumerate(chunks):
            for o in s_peers:
                q, where = slice_of(o), number(o)
                off = pl.multiple_of((first_tile(q) + t0) * LANE, LANE)
                remote(src.at[:, :, pl.ds(off, tn * LANE)], dst_of(pl.ds(t0 * LANE, tn * LANE)), ssem.at[i], rsem.at[i], where).start()
                if i == n_chunk - 1:

                    @pl.when(extra(q))
                    def _():
                        end = pl.multiple_of((first_tile(q) + nt) * LANE, LANE)
                        remote(src.at[:, :, pl.ds(end, LANE)], dst_of(last), ssem.at[n_chunk], rsem.at[n_chunk], where).start()

    send_slices(proj_hbm, lambda part: p_buf.at[:, beta, :, part], psend, precv)
    send_slices(psi_hbm, lambda part: psi_buf.at[:, own_rows, part], ssend, srecv)

    small[0].wait()
    occ_row[:, :32] = occ_in[...]
    occ_buf[me_s] = pltpu.roll(occ_row[...], me_s * 32, 1)
    for o in s_peers:
        remote(occ_buf.at[me_s], occ_buf.at[me_s], osend, orecv, number(o)).start()

    kp = w_buf.shape[1]
    used = (nt + 1) * LANE
    mine = local_copies(0, nt)
    more = local_copies(nt, 1)
    mine[0].wait()
    if_extra(lambda: more[0].wait())

    def clear(at, size):
        mil_buf[:, pl.ds(at, size)] = jnp.zeros((3, size), jnp.int32)
        psi_buf[:, :, pl.ds(at, size)] = jnp.zeros((2, psi_buf.shape[1], size), BF16)
        p_buf[:, :, :, pl.ds(at, size)] = jnp.zeros((2, p_buf.shape[1], PROJ, size), BF16)

    if kp > used:
        clear(used, kp - used)

    @pl.when(jnp.logical_not(extra(me_s)))
    def _():
        clear(nt * LANE, LANE)

    small[1].wait()
    idx = [mil_buf[a : a + 1, :].astype(F32) for a in range(3)]
    co = [(idx[0] * lat_ref[0, a] + idx[1] * lat_ref[1, a] + idx[2] * lat_ref[2, a]) / MILLER for a in range(3)]
    iso = (co[0] * co[0] + co[1] * co[1] + co[2] * co[2]) / 3.0
    rows = list(co)
    for a, b in ((0, 0), (1, 1), (2, 2), (0, 1), (0, 2), (1, 2)):
        prod = co[a] * co[b]
        rows.append(prod - iso if a == b else prod)
    for m, row in enumerate(rows):
        w_buf[m : m + 1, :] = row
    facc[...] = jnp.zeros_like(facc)
    sacc[...] = jnp.zeros_like(sacc)
    acc[...] = jnp.zeros_like(acc)

    mine[1].wait()
    if_extra(lambda: more[1].wait())
    plane = pl.ds(pl.multiple_of(z * n_s, n_s), n_s)

    def pass_on(part, i):
        for o in z_peers:
            remote(p_buf.at[:, plane, :, part], p_buf.at[:, plane, :, part], zsend.at[i], zrecv.at[i], number(o)).start()

    for i, (t0, tn) in enumerate(chunks):
        part = pl.ds(t0 * LANE, tn * LANE)
        with jax.named_scope(f'wp{i}'):
            wait_recv(p_buf.at[:, pl.ds(0, n_s - 1), :, part], precv.at[i])
        pass_on(part, i)
        if i == n_chunk - 1:

            @if_extra
            def _():
                wait_recv(p_buf.at[:, pl.ds(0, n_s - 1), :, last], precv.at[n_chunk])
                pass_on(last, n_chunk)

    mine[2].wait()
    if_extra(lambda: more[2].wait())
    nb = psi_buf.shape[1]
    na = p_buf.shape[1]
    for i, (t0, tn) in enumerate(chunks):
        part = pl.ds(t0 * LANE, tn * LANE)
        with jax.named_scope(f'wz{i}'):
            wait_recv(p_buf.at[:, pl.ds(0, n_s * (nz - 1)), :, part], zrecv.at[i])
        with jax.named_scope(f'wpsi{i}'):
            wait_recv(psi_buf.at[:, pl.ds(0, 32 * (n_s - 1)), part], srecv.at[i])
        if i == n_chunk - 1:

            @if_extra
            def _():
                wait_recv(p_buf.at[:, pl.ds(0, n_s * (nz - 1)), :, last], zrecv.at[n_chunk])
                wait_recv(psi_buf.at[:, pl.ds(0, 32 * (n_s - 1)), last], srecv.at[n_chunk])

            tn = tn + 1
            part = pl.ds(t0 * LANE, tn * LANE)
        rhs = psi_buf[:, :, part].reshape(2 * nb, tn * LANE)
        lhs = p_buf[:, :, :, part].reshape(2 * na * PROJ, tn * LANE)
        acc[...] += lax.dot_general(lhs, rhs, (((1,), (1,)), ((), ())), preferred_element_type=F32)

    np_ = na * PROJ
    b_send[:, 0] = (acc[:np_, :nb] + acc[np_:, nb:]).reshape(na, PROJ, nb).astype(BF16)
    b_send[:, 1] = (acc[:np_, nb:] - acc[np_:, :nb]).reshape(na, PROJ, nb).astype(BF16)

    for o in r_peers:
        remote(b_send.at[number(o) - base], rs_buf.at[me_r], rsend, rrecv, number(o)).start()
    rs_buf[me_r] = b_send[me_r]
    for cp in small[2:]:
        cp.wait()
    wait_recv(occ_buf.at[pl.ds(0, n_s - 1)], orecv)
    occ = jnp.sum(occ_buf[...], axis=0)
    kind = spec_ref[me_r]
    count = cnt_ref[me_r]
    mat = coup_ref[kind]
    act = (lax.broadcasted_iota(jnp.int32, (PROJ, PROJ), 0) < count) & (lax.broadcasted_iota(jnp.int32, (PROJ, PROJ), 1) < count)
    mat = jnp.where(act, mat, 0.0)
    wait_recv(rs_buf.at[pl.ds(0, n_r - 1)], rrecv)
    total = jnp.sum(rs_buf[...].astype(F32), axis=0)
    for h in range(2):
        mixed = jnp.zeros((PROJ, nb), F32)
        for i in range(PROJ):
            mixed = mixed + mat[:, i : i + 1] * total[h, i : i + 1, :]
        uv_buf[h, me_r] = (mixed * occ).astype(BF16)

    for o in r_peers:
        remote(uv_buf.at[:, me_r], uv_buf.at[:, me_r], asend, arecv, number(o)).start()
    wait_recv(uv_buf.at[:, pl.ds(0, n_r - 1)], arecv)

    u = uv_buf[0].reshape(np_, nb)
    v = uv_buf[1].reshape(np_, nb)
    negv[0] = u
    negv[1] = v
    negv[2] = -v

    wide = 256

    def block(i, carry):
        cols = pl.ds(pl.multiple_of(i * wide, wide), wide)
        re = psi_buf[0, :, cols]
        im = psi_buf[1, :, cols]
        dot = functools.partial(jnp.dot, preferred_element_type=F32)
        y_re = dot(negv[0], re) + dot(negv[1], im)
        y_im = dot(negv[0], im) + dot(negv[2], re)
        p_re = p_buf[0, :, :, cols].astype(F32).reshape(np_, wide)
        p_im = p_buf[1, :, :, cols].astype(F32).reshape(np_, wide)
        e_im = (p_re * y_im - p_im * y_re).reshape(na, PROJ, wide)
        e_re = jnp.sum((p_re * y_re + p_im * y_im).reshape(na, PROJ, wide), axis=0)
        for a in range(3):
            t = e_im * w_buf[a : a + 1, cols].reshape(1, 1, wide)
            facc[a] += t[:, :, :LANE] + t[:, :, LANE:]
        for m in range(6):
            t = e_re * w_buf[3 + m : 4 + m, cols]
            sacc[m] += t[:, :LANE] + t[:, LANE:]
        return carry

    lax.fori_loop(0, kp // wide, block, 0)

    lane = lax.broadcasted_iota(jnp.int32, (1, LANE), 1)
    row = jnp.zeros((1, LANE), F32)
    for a in range(3):
        f = jnp.sum(facc[a], axis=1)
        f = jnp.concatenate([jnp.zeros((a * na, LANE), F32), f, jnp.zeros((LANE - (a + 1) * na, LANE), F32)][0 if a else 1 :], axis=0)
        row = row + jnp.sum(f.T, axis=0, keepdims=True)
    for m in range(6):
        row = row + jnp.where(lane == 3 * na + m, jnp.sum(sacc[m], keepdims=True), 0.0)
    tot[me] = row
    for o in all_peers:
        remote(tot.at[me], tot.at[me], fsend, frecv, number(o)).start()
    wait_recv(tot.at[pl.ds(0, n_all - 1)], frecv)
    res = jnp.sum(tot[...], axis=0)
    out_ref[...] = res

    for i, (t0, tn) in enumerate(chunks):
        part = pl.ds(t0 * LANE, tn * LANE)
        wait_send(p_buf.at[:, pl.ds(0, n_s - 1), :, part], psend.at[i])
        wait_send(psi_buf.at[:, pl.ds(0, 32 * (n_s - 1)), part], ssend.at[i])
        wait_send(p_buf.at[:, pl.ds(0, n_s * (nz - 1)), :, part], zsend.at[i])
    for o in s_peers:

        @pl.when(extra(slice_of(o)))
        def _():
            wait_send(p_buf.at[:, 0, :, last], psend.at[n_chunk])
            wait_send(psi_buf.at[:, pl.ds(0, 32), last], ssend.at[n_chunk])

    if_extra(lambda: wait_send(p_buf.at[:, pl.ds(0, n_s * (nz - 1)), :, last], zsend.at[n_chunk]))
    wait_send(occ_buf.at[pl.ds(0, n_s - 1)], osend)
    wait_send(rs_buf.at[pl.ds(0, n_r - 1)], rsend)
    wait_send(uv_buf.at[:, pl.ds(0, n_r - 1)], asend)
    wait_send(tot.at[pl.ds(0, n_all - 1)], fsend)


def finish(dims, na, scales, row_ref, force_ref, stress_ref):
    res = row_ref[...]
    beta = (lax.axis_index("z") * dims[1] + lax.axis_index("yh")) * dims[2] + lax.axis_index("x")
    lane = lax.broadcasted_iota(jnp.int32, (1, LANE), 1)
    own = [jnp.sum(jnp.where(lane == a * na + beta, res, 0.0), axis=1, keepdims=True) for a in range(3)]
    force_ref[...] = jnp.where(lane[:, :3] == 0, own[0], jnp.where(lane[:, :3] == 1, own[1], own[2])) * scales[0]
    i0 = lax.broadcasted_iota(jnp.int32, (3, 3), 0)
    i1 = lax.broadcasted_iota(jnp.int32, (3, 3), 1)
    st = jnp.zeros((3, 3), F32)
    for m, (a, b) in enumerate(((0, 0), (1, 1), (2, 2), (0, 1), (0, 2), (1, 2))):
        val = jnp.sum(jnp.where(lane == 3 * na + m, res, 0.0), axis=1, keepdims=True)
        hit = ((i0 == a) & (i1 == b)) | ((i0 == b) & (i1 == a))
        st = st + jnp.where(hit, val, 0.0)
    stress_ref[...] = st * scales[1]


def body(dims, psi, proj, miller, lattice, occupation, species, proj_count, coupling):
    nz, nyh, nx, nyl, nc = dims
    n_s = nyh * nx
    n_r = n_s * nyl * nc
    bands = psi.shape[1]
    tiles = psi.shape[2] // LANE
    atoms = species.shape[0]
    nt = tiles // n_s
    sizes = []
    left = nt
    for want in (6, 5, 4):
        if left > want:
            sizes.append(want)
            left -= want
    sizes.append(left)
    chunks, at = [], 0
    for n in sizes:
        chunks.append((at, n))
        at += n
    kp = -(-(nt + 1) * LANE // 256) * 256
    nb = n_s * bands
    band_total = nb * nz
    scales = (2.0 / (PROJ * math.sqrt(band_total)), 1.0 / (PROJ * math.sqrt(atoms * band_total)))
    any_spec = pl.BlockSpec(memory_space=pl.ANY)
    vmem = pl.BlockSpec(memory_space=pltpu.VMEM)
    dma = pltpu.SemaphoreType.DMA
    nch = len(chunks)
    row = pl.pallas_call(
        functools.partial(kernel, dims, nt, tiles, tuple(chunks)),
        out_shape=jax.ShapeDtypeStruct((1, LANE), F32),
        in_specs=[any_spec] * 8,
        out_specs=vmem,
        scratch_shapes=[
            pltpu.VMEM((2, nb, kp), BF16),
            pltpu.VMEM((2, atoms, PROJ, kp), BF16),
            pltpu.VMEM((3, kp), jnp.int32),
            pltpu.VMEM((n_s, 1, nb), F32),
            pltpu.VMEM((16, kp), F32),
            pltpu.VMEM((2 * atoms * PROJ, 2 * nb), F32),
            pltpu.VMEM((atoms, 2, PROJ, nb), BF16),
            pltpu.VMEM((n_r, 2, PROJ, nb), BF16),
            pltpu.VMEM((2, n_r, PROJ, nb), BF16),
            pltpu.VMEM((3, atoms * PROJ, nb), BF16),
            pltpu.VMEM((3, atoms, PROJ, LANE), F32),
            pltpu.VMEM((6, PROJ, LANE), F32),
            pltpu.VMEM((nz * n_r, 1, LANE), F32),
            pltpu.SMEM((3, 3), F32), pltpu.SMEM(species.shape, jnp.int32), pltpu.SMEM(species.shape, jnp.int32),
            pltpu.VMEM(coupling.shape, F32), pltpu.VMEM((1, nb), F32), pltpu.VMEM((1, bands), F32),
            dma((8,)), *[dma((nch + 1,))] * 6, dma, dma, dma, dma, dma, dma, dma, dma,
        ],
        compiler_params=pltpu.CompilerParams(collective_id=0, has_side_effects=True, vmem_limit_bytes=58 << 20),
        name="plane_kernel",
    )(psi, proj, miller, lattice, occupation[None], species, proj_count, coupling)
    force, stress = pl.pallas_call(
        functools.partial(finish, dims, atoms, scales),
        out_shape=(jax.ShapeDtypeStruct((1, 3), F32), jax.ShapeDtypeStruct((3, 3), F32)),
        in_specs=[vmem],
        out_specs=(vmem, vmem),
        name="finish",
    )(row)
    return force.T, stress


def solution(mesh, dims=(4, 2, 4, 2, 2)):
    finer = Mesh(mesh.devices.reshape(dims), AXES)
    band, gvec = ("z", "yh", "x"), ("yl", "core")
    in_specs = (P(None, band, gvec), P(None, band, gvec), P(None, gvec), P(), P(band), P(), P(), P())
    return jax.shard_map(functools.partial(body, dims), mesh=finer, in_specs=in_specs, out_specs=(P(None, band), P()), check_vma=False)
```

time: 78.4 us -> 69.5 us (0.89)
  Pallas kernels: 73.7 us -> 68.8 us
  local copies, waits for them, and re-layouts: 3.83 us -> 0 us
    pallas_call x1 -> x2, Pallas kernels: 73.7 us -> 68.8 us  [the longest x1 67.5 us: body(): pl.pallas_call(functools.partial(kernel, dims, nt, tiles, tuple(chunks)),...]
    unnamed x3 -> x0, local copies, waits for them, and re-layouts: 1.81 us -> none
    pallas_call x1 -> x0, local copies, waits for them, and re-layouts: 1.24 us -> none  [body(): pl.pallas_call(functools.partial(kernel, dims, nt, tiles, tuple(chunks),...]
where the time goes in v2:
time: 69.5 us; the launch traced here: 69.4 us
  Pallas kernels  68.8 us (99%)
    pallas_call x1, Pallas kernels, body(): pl.pallas_call(functools.partial(kernel, dims, nt, tiles, tuple(chunks)),...  67.5 us

profile of v2, /device:TPU:1, one launch (start us, length us, event | category | flops | bytes accessed | tf_op | source)
XLA Modules:
  0.0 69.4 jit_solution(11398619401748212038)
XLA Ops:
  0.6 67.5 %plane_kernel.1.row_ref = f32[1,128]{1,0:T(1,128)} custom-call(bf16[2,32,18816]{2,1,0:T(8,128)(2,1)} %psi_hbm.1, bf16[2,8,18816]{2,1,0:T(8,128)(2,1)} %proj_hbm.1, s32[3,18816]{1,0:T(4,128)} %miller_hbm.1, f32[3,3]{1,0:T(4,128)} %lat_hbm.1, f32[1,32]{1,0:T(1,128)} %bitcast.2, s32[32]{0:T(128)} %spec_hbm.1, s32[32]{0:T(128)} %cnt_hbm.1, f32[4,8,8]{2,1,0:T(8,128)} %coup_hbm.1), custom_call_target="tpu_custom_call" | custom-call | tf_op jit(solution)/shard_map/plane_kernel/pallas_call | solution.py:346
  68.2 1.3 %finish.1 = (f32[1,3]{1,0:T(1,128)}, f32[3,3]{1,0:T(4,128)}) custom-call(f32[1,128]{1,0:T(1,128)} %plane_kernel.1.row_ref), custom_call_target="tpu_custom_call" | custom-call | tf_op jit(solution)/shard_map/finish/pallas_call | solution.py:372

commit v3 on v2

v3 whole, which is shorter than its diff:
```python
import functools
import itertools
import math

import jax
import jax.numpy as jnp
from jax import lax
from jax.experimental import pallas as pl
from jax.experimental.pallas import tpu as pltpu
from jax.sharding import Mesh
from jax.sharding import PartitionSpec as P

PROJ = 8
MILLER = 24.0
LANE = 128
HALF = 64
LOGICAL = pl.DeviceIdType.LOGICAL
F32 = jnp.float32
BF16 = jnp.bfloat16
AXES = ("z", "yh", "x", "yl", "core")
STRESS = ((0, 0), (1, 1), (2, 2), (0, 1), (0, 2), (1, 2))


def kernel(
    dims, nt, tiles, p_chunks, phases,
    psi_hbm, proj_hbm, miller_hbm, lat_hbm, occ_hbm, spec_hbm, cnt_hbm, coup_hbm,
    out_ref,
    psi_buf, p_buf, mil_buf, occ_buf, w_buf, lat_ref, spec_ref, cnt_ref, coup_ref, occ_row, occ_in, y_buf, facc, sacc, tot,
    *rest,
):
    n_ph = len(phases)
    per = [rest[i * 5 : i * 5 + 5] for i in range(n_ph)]
    loc_sem, psend, precv, zsend, zrecv, osend, orecv, ssend, srecv, rsend, rrecv, asend, arecv, fsend, frecv = rest[5 * n_ph :]
    nz, nyh, nx, nyl, nc = dims
    n_s = nyh * nx
    n_r = n_s * nyl * nc
    n_all = nz * n_r
    z, yh, x, yl, c = (lax.axis_index(a) for a in AXES)
    me_s = yh * nx + x
    me_r = me_s * (nyl * nc) + yl * nc + c
    me = z * n_r + me_r
    beta = z * n_s + me_s
    na = p_buf.shape[1]
    np_ = na * PROJ
    kp = w_buf.shape[1]

    strides = (n_r, nx * nyl * nc, nyl * nc, nc, 1)
    digits = []
    for at, n, stride in zip((z, yh, x, yl, c), dims, strides):
        digits.append([jnp.where(at + k >= n, at + k - n, at + k) * stride if k else at * stride for k in range(n)])

    def hops(offset):
        dz, a, b, d, e = offset
        return min(dz, nz - dz) + min(b, nx - b) + (2 if a and not d else 1 if a or d else 0)

    def peers(free):
        spans = [range(n) if f else (0,) for n, f in zip(dims, free)]
        offsets = [o for o in itertools.product(*spans) if any(o)]
        return sorted(offsets, key=lambda o: -hops(o))

    def number(offset):
        return sum(digits[i][k] for i, k in enumerate(offset))

    s_peers = peers((0, 1, 1, 0, 0))
    r_peers = peers((0, 1, 1, 1, 1))
    z_peers = peers((1, 0, 0, 0, 0))
    all_peers = peers((1, 1, 1, 1, 1))
    base = digits[0][0]

    def slice_of(offset):
        return (digits[1][offset[1]] + digits[2][offset[2]]) // (nyl * nc)

    def first_tile(q):
        return (q * tiles) // n_s

    def extra(q):
        return first_tile(q + 1) - first_tile(q) > nt

    def remote(src, dst, ssem, rsem, where):
        return pltpu.make_async_remote_copy(src, dst, ssem, rsem, device_id=where, device_id_type=LOGICAL)

    def wait_recv(ref, sem):
        remote(ref, ref, sem, sem, number(s_peers[0])).wait_recv()

    def wait_send(ref, sem):
        remote(ref, ref, sem, sem, number(s_peers[0])).wait_send()

    my_off = pl.multiple_of(first_tile(me_s) * LANE, LANE)
    if_extra = pl.when(extra(me_s))
    last = pl.ds(nt * LANE, LANE)

    def cols(chunk):
        return pl.ds(chunk[0] * LANE, chunk[1] * LANE)

    def local_copies(t0, tn):
        here = pl.ds(pl.multiple_of(my_off + t0 * LANE, LANE), tn * LANE)
        there = pl.ds(t0 * LANE, tn * LANE)
        return [pltpu.make_async_copy(miller_hbm.at[:, here], mil_buf.at[:, there], loc_sem.at[0]),
                pltpu.make_async_copy(proj_hbm.at[:, :, here], p_buf.at[:, beta, :, there], loc_sem.at[1]),
                pltpu.make_async_copy(psi_hbm.at[:, :, :, here], psi_buf.at[:, :, me_s, :, there], loc_sem.at[2])]

    small = [pltpu.make_async_copy(a, b, loc_sem.at[3 + n]) for n, (a, b) in enumerate((
        (occ_hbm, occ_in), (lat_hbm, lat_ref), (spec_hbm, spec_ref), (cnt_hbm, cnt_ref), (coup_hbm, coup_ref)))]

    bar = pltpu.get_barrier_semaphore()
    for o in sorted(z_peers + r_peers, key=lambda o: -hops(o)):
        pl.semaphore_signal(bar, 1, device_id=number(o), device_id_type=LOGICAL)
    occ_row[...] = jnp.zeros_like(occ_row)
    for cp in small + local_copies(0, nt):
        cp.start()

    @if_extra
    def _():
        for cp in local_copies(nt, 1):
            cp.start()

    pl.semaphore_wait(bar, n_r - 1 + nz - 1)

    def send_slices(src, dst_of, chunks, ssem, rsem):
        for i, (t0, tn) in enumerate(chunks):
            for o in s_peers:
                q, where = slice_of(o), number(o)
                off = pl.multiple_of((first_tile(q) + t0) * LANE, LANE)
                remote(src(pl.ds(off, tn * LANE)), dst_of(cols((t0, tn))), ssem(i), rsem(i), where).start()
                if i == 0:

                    @pl.when(extra(q))
                    def _():
                        end = pl.multiple_of((first_tile(q) + nt) * LANE, LANE)
                        remote(src(pl.ds(end, LANE)), dst_of(last), ssem(len(chunks)), rsem(len(chunks)), where).start()

    send_slices(lambda part: proj_hbm.at[:, :, part], lambda part: p_buf.at[:, beta, :, part], p_chunks, lambda i: psend.at[i], lambda i: precv.at[i])
    for h, (g0, gn, chunks) in enumerate(phases):
        send_slices(lambda part: psi_hbm.at[:, pl.ds(g0, gn), :, part], lambda part: psi_buf.at[:, pl.ds(g0, gn), me_s, :, part],
                    chunks, lambda i: ssend.at[h, i], lambda i: srecv.at[h, i])

    lane = lax.broadcasted_iota(jnp.int32, (1, LANE), 1)
    small[0].wait()
    n_g = occ_buf.shape[1]
    occ_row[:, : occ_in.shape[1]] = occ_in[...]
    raw = occ_row[...]
    mine8 = (lane >= me_s * 8) & (lane < me_s * 8 + 8)
    for g in range(n_g):
        occ_buf[me_s, g : g + 1, :] = jnp.where(mine8, pltpu.roll(raw, me_s * 8 + (LANE - 8 * g) % LANE, 1), 0.0)
    for o in s_peers:
        remote(occ_buf.at[me_s], occ_buf.at[me_s], osend, orecv, number(o)).start()

    mine = local_copies(0, nt)
    more = local_copies(nt, 1)
    mine[0].wait()
    if_extra(lambda: more[0].wait())

    def clear(at, size):
        mil_buf[:, pl.ds(at, size)] = jnp.zeros((3, size), jnp.int32)
        psi_buf[:, :, :, :, pl.ds(at, size)] = jnp.zeros((*psi_buf.shape[:4], size), BF16)
        p_buf[:, :, :, pl.ds(at, size)] = jnp.zeros((2, na, PROJ, size), BF16)

    clear((nt + 1) * LANE, kp - (nt + 1) * LANE)

    @pl.when(jnp.logical_not(extra(me_s)))
    def _():
        clear(nt * LANE, LANE)

    small[1].wait()
    idx = [mil_buf[a : a + 1, :].astype(F32) for a in range(3)]
    co = [(idx[0] * lat_ref[0, a] + idx[1] * lat_ref[1, a] + idx[2] * lat_ref[2, a]) / MILLER for a in range(3)]
    iso = (co[0] * co[0] + co[1] * co[1] + co[2] * co[2]) / 3.0
    rows = list(co)
    for a, b in STRESS:
        prod = co[a] * co[b]
        rows.append(prod - iso if a == b else prod)
    for m, row in enumerate(rows):
        w_buf[m : m + 1, :] = row
    facc[...] = jnp.zeros_like(facc)
    sacc[...] = jnp.zeros_like(sacc)

    mine[1].wait()
    if_extra(lambda: more[1].wait())
    n_pc = len(p_chunks)
    up, down = number((1, 0, 0, 0, 0)), number((nz - 1, 0, 0, 0, 0))

    def plane(k):
        return pl.ds(pl.multiple_of(digits[0][k % nz] // n_r * n_s, n_s), n_s)

    def z_own(part, i):
        wait_recv(p_buf.at[:, pl.ds(0, n_s - 1), :, part], precv.at[i])
        ref = p_buf.at[:, plane(0), :, part]
        remote(ref, ref, zsend.at[0, i], zrecv.at[0, i], up).start()
        remote(ref, ref, zsend.at[1, i], zrecv.at[1, i], down).start()

    def z_next(part, i):
        wait_recv(p_buf.at[:, plane(0), :, part], zrecv.at[0, i])
        ref = p_buf.at[0, plane(-1), :, part]
        remote(ref, ref, zsend.at[2, i], zrecv.at[2, i], up).start()
        wait_recv(p_buf.at[:, plane(0), :, part], zrecv.at[1, i])
        ref = p_buf.at[1, plane(1), :, part]
        remote(ref, ref, zsend.at[3, i], zrecv.at[3, i], down).start()

    def z_end(part, i):
        wait_recv(p_buf.at[0, plane(0), :, part], zrecv.at[2, i])
        wait_recv(p_buf.at[1, plane(0), :, part], zrecv.at[3, i])

    def each_chunk(step):
        for i, chunk in enumerate(p_chunks):
            step(cols(chunk), i)
            if i == 0:
                if_extra(lambda: step(last, n_pc))

    each_chunk(z_own)
    each_chunk(z_next)

    mine[2].wait()
    if_extra(lambda: more[2].wait())
    for cp in small[2:]:
        cp.wait()
    kind = spec_ref[me_r]
    count = cnt_ref[me_r]
    act = (lax.broadcasted_iota(jnp.int32, (PROJ, PROJ), 0) < count) & (lax.broadcasted_iota(jnp.int32, (PROJ, PROJ), 1) < count)
    mat = jnp.where(act, coup_ref[kind], 0.0)
    front = lane < HALF
    z_done = [-1]

    def z_arrived(upto):
        while z_done[0] < n_pc - 1 and (z_done[0] < 0 or sum(p_chunks[z_done[0]]) < upto):
            z_done[0] += 1
            i = z_done[0]
            with jax.named_scope(f"wz{i}"):
                z_end(cols(p_chunks[i]), i)
            if i == 0:
                if_extra(lambda: z_end(last, n_pc))

    def gather_chunk(h, i):
        g0, gn, chunks = phases[h]
        acc = per[h][0]
        z_arrived(sum(chunks[i]))
        with jax.named_scope(f"wpsi{h}{i}"):
            wait_recv(psi_buf.at[:, pl.ds(g0, gn), pl.ds(0, n_s - 1), :, cols(chunks[i])], srecv.at[h, i])
        parts = [cols(chunks[i])]
        if i == 0:
            if_extra(lambda: wait_recv(psi_buf.at[:, pl.ds(g0, gn), pl.ds(0, n_s - 1), :, last], srecv.at[h, len(chunks)]))
            parts.append(pl.ds(nt * LANE, kp - nt * LANE))
        total = None if i == 0 else acc[...]
        for part in parts:
            rhs = jnp.concatenate([psi_buf[r, g, :, :, part].reshape(HALF, part.size) for g in range(g0, g0 + gn) for r in range(2)], axis=0)
            lhs = p_buf[:, :, :, part].reshape(2 * np_, part.size)
            term = lax.dot_general(lhs, rhs, (((1,), (1,)), ((), ())), preferred_element_type=F32)
            total = term if total is None else total + term
        acc[...] = total

    def reduce_start(h):
        acc, b_send, rs_buf = per[h][:3]
        for g in range(phases[h][1]):
            tile = pl.ds(g * LANE, LANE)
            low = pltpu.roll(acc[np_:, tile], HALF, 1)
            b_send[:, :, tile] = (acc[:np_, tile] + jnp.where(front, low, -low)).reshape(na, PROJ, LANE).astype(BF16)
        for o in r_peers:
            remote(b_send.at[number(o) - base], rs_buf.at[me_r], rsend.at[h], rrecv.at[h], number(o)).start()
        rs_buf[me_r] = b_send[me_r]

    def mix_and_spread(h):
        rs_buf, uv_buf = per[h][2:4]
        if h == 0:
            wait_recv(occ_buf.at[pl.ds(0, n_s - 1)], orecv)
        with jax.named_scope(f"rs_wait{h}"):
            wait_recv(rs_buf.at[pl.ds(0, n_r - 1)], rrecv.at[h])
        total = jnp.sum(rs_buf[...].astype(F32), axis=0)
        mixed = jnp.zeros_like(total)
        for i in range(PROJ):
            mixed = mixed + mat[:, i : i + 1] * total[i : i + 1, :]
        occ = jnp.sum(occ_buf[...], axis=0)
        occ = occ + pltpu.roll(occ, HALF, 1)
        for g in range(phases[h][1]):
            tile = pl.ds(g * LANE, LANE)
            at = phases[h][0] + g
            uv_buf[me_r, :, tile] = (mixed[:, g * LANE : (g + 1) * LANE] * occ[at : at + 1, :]).astype(BF16)
        for o in r_peers:
            remote(uv_buf.at[me_r], uv_buf.at[me_r], asend.at[h], arecv.at[h], number(o)).start()

    def collect(h):
        uv_buf, left = per[h][3:5]
        with jax.named_scope(f"ag_wait{h}"):
            wait_recv(uv_buf.at[pl.ds(0, n_r - 1)], arecv.at[h])
        uv = uv_buf[...].reshape(np_, phases[h][1] * LANE)
        left[:np_] = uv
        for g in range(phases[h][1]):
            tile = pl.ds(g * LANE, LANE)
            turned = pltpu.roll(uv[:, g * LANE : (g + 1) * LANE].astype(F32), HALF, 1)
            left[np_:, tile] = jnp.where(front, -turned, turned).astype(BF16)

    wide = 256

    def weighted(h, i):
        g0, gn, _ = phases[h]
        part = pl.ds(pl.multiple_of(i * wide, wide), wide)
        rhs = jnp.concatenate([psi_buf[r, g, :, :, part].reshape(HALF, wide) for g in range(g0, g0 + gn) for r in range(2)], axis=0)
        return part, jnp.dot(per[h][4][...], rhs, preferred_element_type=F32)

    def early_block(h, i, carry):
        part, y = weighted(h, i)
        y_buf[:, part] = y if h == 0 else y_buf[:, part] + y
        return carry

    def block(i, carry):
        part, y = weighted(n_ph - 1, i)
        if n_ph > 1:
            y = y + y_buf[:, part]
        y_re, y_im = y[:np_], y[np_:]
        p_re = p_buf[0, :, :, part].astype(F32).reshape(np_, wide)
        p_im = p_buf[1, :, :, part].astype(F32).reshape(np_, wide)
        e_im = (p_re * y_im - p_im * y_re).reshape(na, PROJ, wide)
        e_re = jnp.sum((p_re * y_re + p_im * y_im).reshape(na, PROJ, wide), axis=0)
        for a in range(3):
            t = e_im * w_buf[a : a + 1, part].reshape(1, 1, wide)
            facc[a] += t[:, :, :LANE] + t[:, :, LANE:]
        for m in range(6):
            t = e_re * w_buf[3 + m : 4 + m, part]
            sacc[m] += t[:, :LANE] + t[:, LANE:]
        return carry

    for i in range(len(phases[0][2])):
        gather_chunk(0, i)
    reduce_start(0)
    if n_ph > 1:
        for i in range(len(phases[1][2])):
            gather_chunk(1, i)
        reduce_start(1)
        mix_and_spread(0)
    mix_and_spread(n_ph - 1)
    if n_ph > 1:
        collect(0)
        lax.fori_loop(0, kp // wide, functools.partial(early_block, 0), 0, unroll=UNROLL)
    collect(n_ph - 1)
    lax.fori_loop(0, kp // wide, block, 0, unroll=UNROLL)

    row = jnp.zeros((1, LANE), F32)
    for a in range(3):
        f = jnp.sum(facc[a], axis=1)
        f = jnp.concatenate([jnp.zeros((a * na, LANE), F32), f, jnp.zeros((LANE - (a + 1) * na, LANE), F32)][0 if a else 1 :], axis=0)
        row = row + jnp.sum(f.T, axis=0, keepdims=True)
    for m in range(6):
        row = row + jnp.where(lane == 3 * na + m, jnp.sum(sacc[m], keepdims=True), 0.0)
    tot[me] = row
    for o in all_peers:
        remote(tot.at[me], tot.at[me], fsend, frecv, number(o)).start()
    wait_recv(tot.at[pl.ds(0, n_all - 1)], frecv)
    out_ref[...] = jnp.sum(tot[...], axis=0)

    for i, chunk in enumerate(p_chunks):
        wait_send(p_buf.at[:, pl.ds(0, n_s - 1), :, cols(chunk)], psend.at[i])

    def z_sent(part, i):
        for k in range(4):
            wait_send(p_buf.at[:, plane(0), :, part] if k < 2 else p_buf.at[0, plane(0), :, part], zsend.at[k, i])

    each_chunk(z_sent)
    for h, (g0, gn, chunks) in enumerate(phases):
        for i, chunk in enumerate(chunks):
            wait_send(psi_buf.at[:, pl.ds(g0, gn), pl.ds(0, n_s - 1), :, cols(chunk)], ssend.at[h, i])
        wait_send(per[h][2].at[pl.ds(0, n_r - 1)], rsend.at[h])
        wait_send(per[h][3].at[pl.ds(0, n_r - 1)], asend.at[h])
    for o in s_peers:

        @pl.when(extra(slice_of(o)))
        def _():
            wait_send(p_buf.at[:, 0, :, last], psend.at[n_pc])
            for h, (g0, gn, chunks) in enumerate(phases):
                wait_send(psi_buf.at[:, pl.ds(g0, gn), 0, :, last], ssend.at[h, len(chunks)])

    wait_send(occ_buf.at[pl.ds(0, n_s - 1)], osend)
    wait_send(tot.at[pl.ds(0, n_all - 1)], fsend)


def finish(dims, na, scales, row_ref, force_ref, stress_ref):
    res = row_ref[...]
    beta = (lax.axis_index("z") * dims[1] + lax.axis_index("yh")) * dims[2] + lax.axis_index("x")
    lane = lax.broadcasted_iota(jnp.int32, (1, LANE), 1)
    own = [jnp.sum(jnp.where(lane == a * na + beta, res, 0.0), axis=1, keepdims=True) for a in range(3)]
    force_ref[...] = jnp.where(lane[:, :3] == 0, own[0], jnp.where(lane[:, :3] == 1, own[1], own[2])) * scales[0]
    i0 = lax.broadcasted_iota(jnp.int32, (3, 3), 0)
    i1 = lax.broadcasted_iota(jnp.int32, (3, 3), 1)
    st = jnp.zeros((3, 3), F32)
    for m, (a, b) in enumerate(STRESS):
        val = jnp.sum(jnp.where(lane == 3 * na + m, res, 0.0), axis=1, keepdims=True)
        hit = ((i0 == a) & (i1 == b)) | ((i0 == b) & (i1 == a))
        st = st + jnp.where(hit, val, 0.0)
    stress_ref[...] = st * scales[1]


def cut(total, wants):
    chunks, at = [], 0
    for n in wants:
        if at + n < total:
            chunks.append((at, n))
            at += n
    chunks.append((at, total - at))
    return tuple(chunks)


UNROLL = 5
P_CUT = (4, 6)
SETS = ((2, (10,)), (2, (8, 6)))


def body(dims, psi, proj, miller, lattice, occupation, species, proj_count, coupling):
    nz, nyh, nx, nyl, nc = dims
    n_s = nyh * nx
    n_r = n_s * nyl * nc
    bands = psi.shape[1]
    n_g = bands // 8
    tiles = psi.shape[2] // LANE
    atoms = species.shape[0]
    nt = tiles // n_s
    p_chunks = cut(nt, P_CUT)
    phases, at = [], 0
    for gn, wants in SETS:
        phases.append((at, gn, cut(nt, wants)))
        at += gn
    n_ph = len(phases)
    most = max(len(chunks) for _, _, chunks in phases) + 1
    n_pc = len(p_chunks) + 1
    kp = -(-(nt + 1) * LANE // 256) * 256
    band_total = bands * n_s * nz
    scales = (2.0 / (PROJ * math.sqrt(band_total)), 1.0 / (PROJ * math.sqrt(atoms * band_total)))
    any_spec = pl.BlockSpec(memory_space=pl.ANY)
    vmem = pl.BlockSpec(memory_space=pltpu.VMEM)
    dma = pltpu.SemaphoreType.DMA
    scratch = [
        pltpu.VMEM((2, n_g, n_s, 8, kp), BF16),
        pltpu.VMEM((2, atoms, PROJ, kp), BF16),
        pltpu.VMEM((3, kp), jnp.int32),
        pltpu.VMEM((n_s, n_g, LANE), F32),
        pltpu.VMEM((16, kp), F32),
        pltpu.SMEM((3, 3), F32), pltpu.SMEM(species.shape, jnp.int32), pltpu.SMEM(species.shape, jnp.int32),
        pltpu.VMEM(coupling.shape, F32), pltpu.VMEM((1, LANE), F32), pltpu.VMEM((1, bands), F32),
        pltpu.VMEM((2 * atoms * PROJ, kp), F32),
        pltpu.VMEM((3, atoms, PROJ, LANE), F32),
        pltpu.VMEM((6, PROJ, LANE), F32),
        pltpu.VMEM((nz * n_r, 1, LANE), F32),
    ]
    for _, gn, _ in phases:
        width = gn * LANE
        scratch += [
            pltpu.VMEM((2 * atoms * PROJ, width), F32),
            pltpu.VMEM((atoms, PROJ, width), BF16),
            pltpu.VMEM((n_r, PROJ, width), BF16),
            pltpu.VMEM((n_r, PROJ, width), BF16),
            pltpu.VMEM((2 * atoms * PROJ, width), BF16),
            ]
    scratch += [dma((8,)), *[dma((n_pc,))] * 2, *[dma((4, n_pc))] * 2, dma, dma, *[dma((n_ph, most))] * 2, *[dma((n_ph,))] * 4, dma, dma]
    row = pl.pallas_call(
        functools.partial(kernel, dims, nt, tiles, p_chunks, tuple(phases)),
        out_shape=jax.ShapeDtypeStruct((1, LANE), F32),
        in_specs=[any_spec] * 8,
        out_specs=vmem,
        scratch_shapes=scratch,
        compiler_params=pltpu.CompilerParams(collective_id=0, has_side_effects=True, vmem_limit_bytes=58 << 20),
        name="plane_kernel",
    )(psi.reshape(2, n_g, 8, psi.shape[2]), proj, miller, lattice, occupation[None], species, proj_count, coupling)
    force, stress = pl.pallas_call(
        functools.partial(finish, dims, atoms, scales),
        out_shape=(jax.ShapeDtypeStruct((1, 3), F32), jax.ShapeDtypeStruct((3, 3), F32)),
        in_specs=[vmem],
        out_specs=(vmem, vmem),
        name="finish",
    )(row)
    return force.T, stress


def solution(mesh, dims=(4, 2, 4, 2, 2)):
    finer = Mesh(mesh.devices.reshape(dims), AXES)
    band, gvec = ("z", "yh", "x"), ("yl", "core")
    in_specs = (P(None, band, gvec), P(None, band, gvec), P(None, gvec), P(), P(band), P(), P(), P())
    return jax.shard_map(functools.partial(body, dims), mesh=finer, in_specs=in_specs, out_specs=(P(None, band), P()), check_vma=False)
```

time: 69.5 us -> 68 us (0.978)
  Pallas kernels: 68.8 us -> 67.3 us
    pallas_call x1, Pallas kernels: 67.5 us -> 66 us  [body(): pl.pallas_call(functools.partial(kernel, dims, nt, tiles, p_chunks, tuple...]
where the time goes in v3:
time: 68 us; the launch traced here: 67.9 us
  Pallas kernels  67.3 us (99%)
    pallas_call x1, Pallas kernels, body(): pl.pallas_call(functools.partial(kernel, dims, nt, tiles, p_chunks, tuple...  66 us

profile of v3, /device:TPU:1, one launch (start us, length us, event | category | flops | bytes accessed | tf_op | source)
XLA Modules:
  0.0 67.9 jit_solution(13393615789990534049)
XLA Ops:
  0.6 66.0 %plane_kernel.1.row_ref = f32[1,128]{1,0:T(1,128)} custom-call(bf16[2,4,8,18816]{3,2,1,0:T(8,128)(2,1)} %bitcast.3, bf16[2,8,18816]{2,1,0:T(8,128)(2,1)} %proj_hbm.1, s32[3,18816]{1,0:T(4,128)} %miller_hbm.1, f32[3,3]{1,0:T(4,128)} %lat_hbm.1, f32[1,32]{1,0:T(1,128)} %bitcast.4, s32[32]{0:T(128)} %spec_hbm.1, s32[32]{0:T(128)} %cnt_hbm.1, f32[4,8,8]{2,1,0:T(8,128)} %coup_hbm.1), custom_call_target="tpu_custom_call" | custom-call | tf_op jit(solution)/shard_map/plane_kernel/pallas_call | solution.py:450
  66.6 1.3 %finish.1 = (f32[1,3]{1,0:T(1,128)}, f32[3,3]{1,0:T(4,128)}) custom-call(f32[1,128]{1,0:T(1,128)} %plane_kernel.1.row_ref), custom_call_target="tpu_custom_call" | custom-call | tf_op jit(solution)/shard_map/finish/pallas_call | solution.py:459

commit v4 on v3

--- a/solution.py
+++ b/solution.py
@@ -25,7 +25,7 @@
     dims, nt, tiles, p_chunks, phases,
     psi_hbm, proj_hbm, miller_hbm, lat_hbm, occ_hbm, spec_hbm, cnt_hbm, coup_hbm,
     out_ref,
-    psi_buf, p_buf, mil_buf, occ_buf, w_buf, lat_ref, spec_ref, cnt_ref, coup_ref, occ_row, occ_in, y_buf, facc, sacc, tot,
+    psi_buf, p_buf, mil_buf, occ_buf, w_buf, lat_ref, spec_ref, cnt_ref, coup_ref, occ_row, occ_in, p_wide, facc, sacc, tot,
     *rest,
 ):
     n_ph = len(phases)
@@ -295,18 +295,10 @@
         rhs = jnp.concatenate([psi_buf[r, g, :, :, part].reshape(HALF, wide) for g in range(g0, g0 + gn) for r in range(2)], axis=0)
         return part, jnp.dot(per[h][4][...], rhs, preferred_element_type=F32)
 
-    def early_block(h, i, carry):
+    def block(h, i, carry):
         part, y = weighted(h, i)
-        y_buf[:, part] = y if h == 0 else y_buf[:, part] + y
-        return carry
-
-    def block(i, carry):
-        part, y = weighted(n_ph - 1, i)
-        if n_ph > 1:
-            y = y + y_buf[:, part]
         y_re, y_im = y[:np_], y[np_:]
-        p_re = p_buf[0, :, :, part].astype(F32).reshape(np_, wide)
-        p_im = p_buf[1, :, :, part].astype(F32).reshape(np_, wide)
+        p_re, p_im = p_wide[0, :, part], p_wide[1, :, part]
         e_im = (p_re * y_im - p_im * y_re).reshape(na, PROJ, wide)
         e_re = jnp.sum((p_re * y_re + p_im * y_im).reshape(na, PROJ, wide), axis=0)
         for a in range(3):
@@ -320,6 +312,7 @@
     for i in range(len(phases[0][2])):
         gather_chunk(0, i)
     reduce_start(0)
+    p_wide[...] = p_buf[...].reshape(2, np_, kp).astype(F32)
     if n_ph > 1:
         for i in range(len(phases[1][2])):
             gather_chunk(1, i)
@@ -328,9 +321,9 @@
     mix_and_spread(n_ph - 1)
     if n_ph > 1:
         collect(0)
-        lax.fori_loop(0, kp // wide, functools.partial(early_block, 0), 0, unroll=UNROLL)
+        lax.fori_loop(0, kp // wide, functools.partial(block, 0), 0, unroll=UNROLL)
     collect(n_ph - 1)
-    lax.fori_loop(0, kp // wide, block, 0, unroll=UNROLL)
+    lax.fori_loop(0, kp // wide, functools.partial(block, n_ph - 1), 0, unroll=UNROLL)
 
     row = jnp.zeros((1, LANE), F32)
     for a in range(3):
@@ -398,7 +391,7 @@
 
 UNROLL = 5
 P_CUT = (4, 6)
-SETS = ((2, (10,)), (2, (8, 6)))
+SETS = ((2, (10,)), (2, (8, 8)))
 
 
 def body(dims, psi, proj, miller, lattice, occupation, species, proj_count, coupling):
@@ -432,7 +425,7 @@
         pltpu.VMEM((16, kp), F32),
         pltpu.SMEM((3, 3), F32), pltpu.SMEM(species.shape, jnp.int32), pltpu.SMEM(species.shape, jnp.int32),
         pltpu.VMEM(coupling.shape, F32), pltpu.VMEM((1, LANE), F32), pltpu.VMEM((1, bands), F32),
-        pltpu.VMEM((2 * atoms * PROJ, kp), F32),
+        pltpu.VMEM((2, atoms * PROJ, kp), F32),
         pltpu.VMEM((3, atoms, PROJ, LANE), F32),
         pltpu.VMEM((6, PROJ, LANE), F32),
         pltpu.VMEM((nz * n_r, 1, LANE), F32),
@@ -449,7 +442,7 @@
     scratch += [dma((8,)), *[dma((n_pc,))] * 2, *[dma((4, n_pc))] * 2, dma, dma, *[dma((n_ph, most))] * 2, *[dma((n_ph,))] * 4, dma, dma]
     row = pl.pallas_call(
         functools.partial(kernel, dims, nt, tiles, p_chunks, tuple(phases)),
-        out_shape=jax.ShapeDtypeStruct((1, LANE), F32),
+        out_shape=pltpu.VMEM((1, LANE), F32),
         in_specs=[any_spec] * 8,
         out_specs=vmem,
         scratch_shapes=scratch,
@@ -462,7 +455,7 @@
         in_specs=[vmem],
         out_specs=(vmem, vmem),
         name="finish",
-    )(row)
+    )(pltpu.with_memory_space_constraint(row, pltpu.VMEM))
     return force.T, stress
 
 

time: 68 us -> 66.5 us (0.978)
  Pallas kernels: 67.3 us -> 65.7 us
    pallas_call x1, Pallas kernels: 66 us -> 65.1 us  [body(): pl.pallas_call(functools.partial(kernel, dims, nt, tiles, p_chunks, tuple...]
where the time goes in v4:
time: 66.5 us; the launch traced here: 66.4 us
  Pallas kernels  65.7 us (99%)
    pallas_call x1, Pallas kernels, body(): pl.pallas_call(functools.partial(kernel, dims, nt, tiles, p_chunks, tuple...  65.1 us

profile of v4, /device:TPU:1, one launch (start us, length us, event | category | flops | bytes accessed | tf_op | source)
XLA Modules:
  0.0 66.4 jit_solution(17190124858340738653)
XLA Ops:
  0.6 65.1 %plane_kernel.1.row_ref = f32[1,128]{1,0:T(1,128)S(1)} custom-call(bf16[2,4,8,18816]{3,2,1,0:T(8,128)(2,1)} %bitcast.3, bf16[2,8,18816]{2,1,0:T(8,128)(2,1)} %proj_hbm.1, s32[3,18816]{1,0:T(4,128)} %miller_hbm.1, f32[3,3]{1,0:T(4,128)} %lat_hbm.1, f32[1,32]{1,0:T(1,128)} %bitcast.4, s32[32]{0:T(128)} %spec_hbm.1, s32[32]{0:T(128)} %cnt_hbm.1, ...), custom_call_target="tpu_custom_call" | custom-call | tf_op jit(solution)/shard_map/plane_kernel/pallas_call | solution.py:443
  65.7 0.7 %finish.1 = (f32[1,3]{1,0:T(1,128)}, f32[3,3]{1,0:T(4,128)}) custom-call(f32[1,128]{1,0:T(1,128)S(1)} %plane_kernel.1.row_ref), custom_call_target="tpu_custom_call" | custom-call | tf_op jit(solution)/shard_map/finish/pallas_call | solution.py:452

commit v5 on v4

--- a/solution.py
+++ b/solution.py
@@ -71,7 +71,7 @@
         return (digits[1][offset[1]] + digits[2][offset[2]]) // (nyl * nc)
 
     def first_tile(q):
-        return (q * tiles) // n_s
+        return (q * tiles + (n_s // 2) * c + (n_s // 4) * yl) // n_s
 
     def extra(q):
         return first_tile(q + 1) - first_tile(q) > nt

time: 66.5 us -> 65.8 us (0.989)
  no operation moved by 1% of the time
where the time goes in v5:
time: 65.8 us; the launch traced here: 65.7 us
  Pallas kernels  65.1 us (99%)
    pallas_call x1, Pallas kernels, body(): pl.pallas_call(functools.partial(kernel, dims, nt, tiles, p_chunks, tuple...  64.4 us

profile of v5, /device:TPU:1, one launch (start us, length us, event | category | flops | bytes accessed | tf_op | source)
XLA Modules:
  0.0 65.7 jit_solution(2169893738437961382)
XLA Ops:
  0.6 64.4 %plane_kernel.1.row_ref = f32[1,128]{1,0:T(1,128)S(1)} custom-call(bf16[2,4,8,18816]{3,2,1,0:T(8,128)(2,1)} %bitcast.3, bf16[2,8,18816]{2,1,0:T(8,128)(2,1)} %proj_hbm.1, s32[3,18816]{1,0:T(4,128)} %miller_hbm.1, f32[3,3]{1,0:T(4,128)} %lat_hbm.1, f32[1,32]{1,0:T(1,128)} %bitcast.4, s32[32]{0:T(128)} %spec_hbm.1, s32[32]{0:T(128)} %cnt_hbm.1, ...), custom_call_target="tpu_custom_call" | custom-call | tf_op jit(solution)/shard_map/plane_kernel/pallas_call | solution.py:443
  65.0 0.7 %finish.1 = (f32[1,3]{1,0:T(1,128)}, f32[3,3]{1,0:T(4,128)}) custom-call(f32[1,128]{1,0:T(1,128)S(1)} %plane_kernel.1.row_ref), custom_call_target="tpu_custom_call" | custom-call | tf_op jit(solution)/shard_map/finish/pallas_call | solution.py:452

commit v6 on v5

--- a/solution.py
+++ b/solution.py
@@ -252,7 +252,7 @@
         for g in range(phases[h][1]):
             tile = pl.ds(g * LANE, LANE)
             low = pltpu.roll(acc[np_:, tile], HALF, 1)
-            b_send[:, :, tile] = (acc[:np_, tile] + jnp.where(front, low, -low)).reshape(na, PROJ, LANE).astype(BF16)
+            b_send[:, :, tile] = (acc[:np_, tile] + jnp.where(front, low, -low)).reshape(na, PROJ, LANE)
         for o in r_peers:
             remote(b_send.at[number(o) - base], rs_buf.at[me_r], rsend.at[h], rrecv.at[h], number(o)).start()
         rs_buf[me_r] = b_send[me_r]
@@ -263,7 +263,7 @@
             wait_recv(occ_buf.at[pl.ds(0, n_s - 1)], orecv)
         with jax.named_scope(f"rs_wait{h}"):
             wait_recv(rs_buf.at[pl.ds(0, n_r - 1)], rrecv.at[h])
-        total = jnp.sum(rs_buf[...].astype(F32), axis=0)
+        total = jnp.sum(rs_buf[...], axis=0)
         mixed = jnp.zeros_like(total)
         for i in range(PROJ):
             mixed = mixed + mat[:, i : i + 1] * total[i : i + 1, :]
@@ -389,7 +389,7 @@
     return tuple(chunks)
 
 
-UNROLL = 5
+UNROLL = 10
 P_CUT = (4, 6)
 SETS = ((2, (10,)), (2, (8, 8)))
 
@@ -434,8 +434,8 @@
         width = gn * LANE
         scratch += [
             pltpu.VMEM((2 * atoms * PROJ, width), F32),
-            pltpu.VMEM((atoms, PROJ, width), BF16),
-            pltpu.VMEM((n_r, PROJ, width), BF16),
+            pltpu.VMEM((atoms, PROJ, width), F32),
+            pltpu.VMEM((n_r, PROJ, width), F32),
             pltpu.VMEM((n_r, PROJ, width), BF16),
             pltpu.VMEM((2 * atoms * PROJ, width), BF16),
             ]

time: 65.8 us -> 66.5 us (1.011)
  Pallas kernels: 65.1 us -> 65.8 us
    pallas_call x1, Pallas kernels: 64.4 us -> 65.1 us  [body(): pl.pallas_call(functools.partial(kernel, dims, nt, tiles, p_chunks, tuple...]
where the time goes in v6:
time: 66.5 us; the launch traced here: 66.4 us
  Pallas kernels  65.8 us (99%)
    pallas_call x1, Pallas kernels, body(): pl.pallas_call(functools.partial(kernel, dims, nt, tiles, p_chunks, tuple...  65.1 us

profile of v6, /device:TPU:1, one launch (start us, length us, event | category | flops | bytes accessed | tf_op | source)
XLA Modules:
  0.0 66.4 jit_solution(6504974461255762967)
XLA Ops:
  0.6 65.1 %plane_kernel.1.row_ref = f32[1,128]{1,0:T(1,128)S(1)} custom-call(bf16[2,4,8,18816]{3,2,1,0:T(8,128)(2,1)} %bitcast.3, bf16[2,8,18816]{2,1,0:T(8,128)(2,1)} %proj_hbm.1, s32[3,18816]{1,0:T(4,128)} %miller_hbm.1, f32[3,3]{1,0:T(4,128)} %lat_hbm.1, f32[1,32]{1,0:T(1,128)} %bitcast.4, s32[32]{0:T(128)} %spec_hbm.1, s32[32]{0:T(128)} %cnt_hbm.1, ...), custom_call_target="tpu_custom_call" | custom-call | tf_op jit(solution)/shard_map/plane_kernel/pallas_call | solution.py:443
  65.7 0.7 %finish.1 = (f32[1,3]{1,0:T(1,128)}, f32[3,3]{1,0:T(4,128)}) custom-call(f32[1,128]{1,0:T(1,128)S(1)} %plane_kernel.1.row_ref), custom_call_target="tpu_custom_call" | custom-call | tf_op jit(solution)/shard_map/finish/pallas_call | solution.py:452
